TPU v7x, 8 devices: a whole 2x2x1 slice. The times are simulated.
8 devices in a mesh: dp: 1 (over z), tp: 2 (over y), pp: 4 (over x, core).
Axes of the slice: x: 2, y: 2, z: 1, core: 2. Of those that a mesh axis runs over, the one named last changes fastest.
Arguments:
- hidden: bfloat16 [2, 128, 2048], P('dp')
- positions: int32 [2, 128], P('dp')
- key_cache: bfloat16 [4, 2, 128, 32, 32, 64], P('pp', 'dp', None, 'tp')
- value_cache: bfloat16 [4, 2, 128, 32, 32, 64], P('pp', 'dp', None, 'tp')
- attn_norm: bfloat16 [4, 2048], P('pp')
- w_query: bfloat16 [4, 2048, 2048], P('pp', None, 'tp')
- w_key: bfloat16 [4, 2048, 2048], P('pp', None, 'tp')
- w_value: bfloat16 [4, 2048, 2048], P('pp', None, 'tp')
- w_out: bfloat16 [4, 2048, 2048], P('pp', 'tp')
- mlp_norm: bfloat16 [4, 2048], P('pp')
- w_gate: bfloat16 [4, 2048, 8192], P('pp', None, 'tp')
- w_up: bfloat16 [4, 2048, 8192], P('pp', None, 'tp')
- w_down: bfloat16 [4, 8192, 2048], P('pp', 'tp')
Outputs:
- output 1: bfloat16 [2, 128, 2048], P('dp')
- output 2: bfloat16 [4, 2, 128, 32, 32, 64], P('pp', 'dp', None, 'tp')
- output 3: bfloat16 [4, 2, 128, 32, 32, 64], P('pp', 'dp', None, 'tp')
All inputs are finite; a program needn't handle non-finite values.
Results may differ from a plain program's by a relative error of at most 0.02.
Values are sent between devices in bfloat16 or wider.
A program may use at most 1 GiB of HBM per device.

v0:
```python
import math
import jax
import jax.numpy as jnp
from jax import lax
from jax.sharding import PartitionSpec as P

ROPE_THETA = 500000.0
SCALE_FACTOR = 8.0
LOW_FACTOR = 1.0
HIGH_FACTOR = 4.0
ORIG_CONTEXT = 8192.0
NORM_EPS = 1e-5


def rope_freqs(head_dim):
    freq_index = jnp.arange(head_dim // 2, dtype=jnp.float32)
    base_freq = ROPE_THETA ** (-2.0 * freq_index / head_dim)
    wave_len = 2.0 * math.pi / base_freq
    smooth_t = (ORIG_CONTEXT / wave_len - LOW_FACTOR) / (HIGH_FACTOR - LOW_FACTOR)
    mixed_freq = (1.0 - smooth_t) * base_freq / SCALE_FACTOR + smooth_t * base_freq
    long_freq = jnp.where(wave_len > ORIG_CONTEXT / LOW_FACTOR, base_freq / SCALE_FACTOR, mixed_freq)
    return jnp.where(wave_len < ORIG_CONTEXT / HIGH_FACTOR, base_freq, long_freq)


def rms_norm(values, gain_vec):
    values_f = values.astype(jnp.float32)
    inv_rms = lax.rsqrt(jnp.mean(values_f * values_f, axis=-1, keepdims=True) + NORM_EPS)
    return (values_f * inv_rms * gain_vec.astype(jnp.float32)).astype(jnp.bfloat16)


def rotate(values_f, cosine, sine_t):
    half_dim = values_f.shape[-1] // 2
    first_half = values_f[..., :half_dim]
    second_half = values_f[..., half_dim:]
    return jnp.concatenate([first_half * cosine - second_half * sine_t, second_half * cosine + first_half * sine_t], axis=-1)


def attention_part(tokens, key_cache, value_cache, positions, params):
    gain_attn, w_query, w_key, w_value, w_out = params
    n_groups, n_batch, kv_local, seq_len, head_dim = key_cache.shape
    heads_local = w_query.shape[-1] // head_dim
    gqa_size = heads_local // kv_local
    angles = positions.astype(jnp.float32)[..., None] * rope_freqs(head_dim)
    cosine = jnp.cos(angles)
    sine_t = jnp.sin(angles)
    normed = rms_norm(tokens, gain_attn)
    query_f = jnp.einsum("mbd,dh->mbh", normed, w_query, preferred_element_type=jnp.float32)
    query_h = rotate(query_f.reshape(n_groups, n_batch, kv_local, gqa_size, head_dim), cosine[:, :, None, None, :], sine_t[:, :, None, None, :]).astype(jnp.bfloat16)
    key_f = jnp.einsum("mbd,dh->mbh", normed, w_key, preferred_element_type=jnp.float32)
    key_new = rotate(key_f.reshape(n_groups, n_batch, kv_local, head_dim), cosine[:, :, None, :], sine_t[:, :, None, :]).astype(jnp.bfloat16)
    value_new = jnp.einsum("mbd,dh->mbh", normed, w_value, preferred_element_type=jnp.float32).astype(jnp.bfloat16).reshape(n_groups, n_batch, kv_local, head_dim)
    seq_rows = jnp.arange(seq_len)
    row_hit = (seq_rows == positions[..., None])[:, :, None, :, None]
    key_cache = jnp.where(row_hit, key_new[:, :, :, None, :], key_cache)
    value_cache = jnp.where(row_hit, value_new[:, :, :, None, :], value_cache)
    scores = jnp.einsum("mbkgd,mbksd->mbkgs", query_h, key_cache, preferred_element_type=jnp.float32) * head_dim ** -0.5
    visible = (seq_rows <= positions[..., None])[:, :, None, None, :]
    attn_probs = jax.nn.softmax(jnp.where(visible, scores, -jnp.inf), axis=-1).astype(jnp.bfloat16)
    attn_vals = jnp.einsum("mbkgs,mbksd->mbkgd", attn_probs, value_cache, preferred_element_type=jnp.float32).astype(jnp.bfloat16).reshape(n_groups, n_batch, heads_local * head_dim)
    attn_partial = jnp.einsum("mbh,hd->mbd", attn_vals, w_out, preferred_element_type=jnp.float32).astype(jnp.bfloat16)
    return attn_partial, key_cache, value_cache


def mlp_part(mid_state, gain_mlp, w_gate, w_up, w_down):
    normed_mlp = rms_norm(mid_state, gain_mlp)
    gate_f = jnp.einsum("mbd,df->mbf", normed_mlp, w_gate, preferred_element_type=jnp.float32)
    up_f = jnp.einsum("mbd,df->mbf", normed_mlp, w_up, preferred_element_type=jnp.float32)
    act_bf = (jax.nn.silu(gate_f) * up_f).astype(jnp.bfloat16)
    return jnp.einsum("mbf,fd->mbd", act_bf, w_down, preferred_element_type=jnp.float32).astype(jnp.bfloat16)


def solution(mesh):
    n_stages = mesh.shape["pp"]
    cache_spec = P("pp", "dp", None, "tp", None, None)
    col_spec = P("pp", None, "tp")
    row_spec = P("pp", "tp", None)
    gain_spec = P("pp", None)
    in_specs = (P("dp", None, None), P("dp", None), cache_spec, cache_spec, gain_spec, col_spec, col_spec, col_spec, row_spec, gain_spec, col_spec, col_spec, row_spec)
    out_specs = (P("dp", None, None), cache_spec, cache_spec)

    def per_device(hidden, positions, key_cache, value_cache, attn_norm, w_query, w_key, w_value, w_out, mlp_norm, w_gate, w_up, w_down):
        stage_idx = lax.axis_index("pp")
        attn_params = (attn_norm[0], w_query[0], w_key[0], w_value[0], w_out[0])
        gain_mlp = mlp_norm[0]
        gate_w = w_gate[0]
        up_w = w_up[0]
        down_w = w_down[0]

        def attn_run(carry_in):
            state_in, key_in, value_in = carry_in
            return attention_part(state_in, key_in, value_in, positions, attn_params)

        def attn_skip(carry_in):
            state_in, key_in, value_in = carry_in
            return jnp.zeros_like(state_in), key_in, value_in

        def mlp_run(mid_in):
            return mlp_part(mid_in, gain_mlp, gate_w, up_w, down_w)

        def mlp_skip(mid_in):
            return jnp.zeros_like(mid_in)

        state_h = hidden
        key_local = key_cache[0]
        value_local = value_cache[0]
        for step_idx in range(n_stages):
            active = stage_idx == step_idx
            attn_partial, key_local, value_local = lax.cond(active, attn_run, attn_skip, (state_h, key_local, value_local))
            attn_out = lax.psum(attn_partial, "tp")
            mid_state = (state_h.astype(jnp.float32) + attn_out.astype(jnp.float32)).astype(jnp.bfloat16)
            mlp_out = lax.psum(lax.cond(active, mlp_run, mlp_skip, mid_state), "tp")
            state_h = (mid_state.astype(jnp.float32) + mlp_out.astype(jnp.float32)).astype(jnp.bfloat16)
            if step_idx + 1 < n_stages:
                state_h = lax.ppermute(state_h, "pp", [(step_idx, step_idx + 1)])
        final_state = lax.psum(state_h, "pp")
        return final_state, key_local[None], value_local[None]

    return jax.shard_map(per_device, mesh=mesh, in_specs=in_specs, out_specs=out_specs, check_vma=False)
```

profile of v0, /device:TPU:0, one launch (start us, length us, event | category | flops | bytes accessed | tf_op | source)
XLA Modules:
  0.0 976.9 jit_solution(13419527865440863689)
XLA Ops:
  7.2 45.9 %copy.76 = bf16[1,2,128,16,32,64]{5,4,3,2,1,0:T(8,128)(2,1)} copy(bf16[1,2,128,16,32,64]{2,5,4,3,1,0:T(8,128)(2,1)} %param.31) | data formatting | bytes 33554432 | tf_op args[2]
  53.2 46.0 %copy.77 = bf16[1,2,128,16,32,64]{5,4,3,2,1,0:T(8,128)(2,1)} copy(bf16[1,2,128,16,32,64]{2,5,4,3,1,0:T(8,128)(2,1)} %param.32) | data formatting | bytes 33554432 | tf_op args[3]
  99.2 92.7 %conditional.8 = (bf16[2,128,2048]{2,1,0:T(8,128)(2,1)}, bf16[2,128,16,32,64]{4,3,2,1,0:T(8,128)(2,1)}, bf16[2,128,16,32,64]{4,3,2,1,0:T(8,128)(2,1)}) conditional(s32[]{:T(128)} %convert_element_type.289, (bf16[2,128,16,32,64]{4,3,2,1,0:T(8,128)(2,1)}, bf16[2,128,16,32,64]{4,3,2,1,0:T(8,128)(2,1)}) %tuple.142, (s32[2,128]{1,0:T(2,128)S(1)}, ...), branch_computations={%region_0.0_spmd, %region_1.5_spmd} | conditional | flops 4375350272 | bytes 119839056 | solution.py:108
  99.3 0.3 fusion.133
  99.6 4.1 fusion.126
  103.7 0.2 multiply_cosine_fusion
  103.9 0.1 subtract_convert_fusion
  104.1 0.8 copy.51
  104.9 4.0 fusion.128
  108.9 0.1 fusion.148
  109.1 0.1 maximum_convert_fusion
  109.2 2.1 copy.136
  111.3 0.1 copy.49
  111.4 24.7 %multiply_reduce_fusion.1 = (f32[2,128,16,32]{3,2,1,0:T(8,128)S(1)}, bf16[2,128,16,32,64]{4,3,2,1,0:T(8,128)(2,1)}) fusion(f32[2,128,16,64]{3,2,1,0:T(8,128)} %copy.136, bf16[2,128,16,32,64]{4,3,2,1,0:T(8,128)(2,1)} %get-tuple-element.147, bf16[2,128,16,64]{3,2,1,0:T(8,128)(2,1)S(1)} %copy.51, pred[2,128,32]{2,1,0:T(8,128)(4,1)S(1)} %copy.49), kind=kLoop, calls=%fused_computation.83 | loop fusion | flops 33423360 | bytes 35659776 | tf_op jit(solution)/shard_map/cond
  136.1 1.6 copy.87
  137.7 2.0 fusion.143
  139.7 2.0 copy.137
  141.7 4.3 fusion.136
  146.0 2.0 copy.52
  148.0 1.8 copy.53
  149.8 35.1 %multiply_reduce_fusion = (bf16[2,128,16,64]{3,2,1,0:T(8,128)(2,1)}, bf16[2,128,16,32,64]{4,3,2,1,0:T(8,128)(2,1)}) fusion(f32[2,128,16,32]{3,2,1,0:T(8,128)S(1)} %copy.137, bf16[2,128,16,32,64]{4,3,2,1,0:T(8,128)(2,1)} %get-tuple-element.149, bf16[2,128,16,64]{3,2,1,0:T(8,128)(2,1)S(1)} %copy.53, pred[2,128,32]{2,1,0:T(8,128)(4,1)S(1)} %copy.49), kind=kLoop, calls=%fused_computation.82 | loop fusion | flops 33292288 | bytes 35135488 | tf_op jit(solution)/shard_map/cond
  185.0 2.0 copy.92
  187.0 4.4 fusion.130
  192.0 36.2 %all-reduce.10.cloned.1.call-done = bf16[2,128,2048]{2,1,0:T(8,128)(2,1)} async-done(((bf16[2,128,2048]{2,1,0:T(8,128)(2,1)}), bf16[2,128,2048]{2,1,0:T(8,128)(2,1)}) %all-reduce.10.cloned.1.call-update) | async-done | bytes 1048592 | tf_op jit(solution)/shard_map/psum | solution.py:109
  228.3 1.9 add_convert_fusion.15
  230.2 27.2 %conditional.9 = (bf16[2,128,2048]{2,1,0:T(8,128)(2,1)S(1)}) conditional(s32[]{:T(128)} %convert_element_type.289, () %tuple.66, (bf16[2,128,2048]{2,1,0:T(8,128)(2,1)S(1)}, bf16[2048]{0:T(1024)(128)(2,1)S(1)}, bf16[2048,4096]{1,0:T(8,128)(2,1)}, bf16[2048,4096]{1,0:T(8,128)(2,1)}, bf16[4096,2048]{1,0:T(8,128)(2,1)}) %tuple.161), branch_computations={%region_6.7_spmd, %region_7.9_spmd} | conditional | flops 12897486848 | bytes 62948360 | solution.py:111
  230.2 0.3 fusion.22
  230.5 10.3 %fusion.4 = f32[2,128,4096]{2,1,0:T(8,128)} fusion(bf16[2048,4096]{1,0:T(8,128)(2,1)} %get-tuple-element.153, bf16[2,128,2048]{2,1,0:T(8,128)(2,1)S(1)} %get-tuple-element.151, f32[2048]{0:T(1024)S(1)} %convert_element_type.217, f32[2,128]{1,0:T(2,128)S(1)} %add_rsqrt_fusion), kind=kOutput, calls=%fused_computation.4 | convolution fusion | flops 4297064448 | bytes 22029312 | tf_op jit(solution)/shard_map/cond/branch_1_fun/mbd,df->mbf/dot_general | solution.py:66
  240.8 16.6 %fusion.17 = bf16[2,128,2048]{2,1,0:T(8,128)(2,1)S(1)} fusion(bf16[4096,2048]{1,0:T(8,128)(2,1)} %get-tuple-element.155, bf16[2048,4096]{1,0:T(8,128)(2,1)} %get-tuple-element.154, f32[2,128,4096]{2,1,0:T(8,128)} %fusion.4, bf16[2,128,2048]{2,1,0:T(8,128)(2,1)S(1)} %get-tuple-element.151, f32[2048]{0:T(1024)S(1)} %convert_element_type.217, ...), kind=kOutput, calls=%fused_computation.13 | convolution fusion | flops 8598847488 | bytes 39855104 | tf_op jit(solution)/shard_map/cond/branch_1_fun/mbf,fd->mbd/dot_general | solution.py:69
  257.5 1.0 copy-done.3
  258.5 33.3 %all-reduce.12.cloned.1.call-done = bf16[2,128,2048]{2,1,0:T(8,128)(2,1)} async-done(((bf16[2,128,2048]{2,1,0:T(8,128)(2,1)}), bf16[2,128,2048]{2,1,0:T(8,128)(2,1)}) %all-reduce.12.cloned.1.call-update) | async-done | bytes 1048592 | tf_op jit(solution)/shard_map/psum | solution.py:111
  291.8 1.6 add_convert_fusion.14
  293.4 2.5 collective-permute-start
  295.9 1.3 collective-permute-done
  297.2 6.7 conditional.10
  297.2 1.1 broadcast.668
  303.9 116.0 %all-reduce.14.cloned.1.call-done = bf16[2,128,2048]{2,1,0:T(8,128)(2,1)} async-done(((bf16[2,128,2048]{2,1,0:T(8,128)(2,1)}), bf16[2,128,2048]{2,1,0:T(8,128)(2,1)}) %all-reduce.14.cloned.1.call-update) | async-done | bytes 1048592 | tf_op jit(solution)/shard_map/psum | solution.py:109
  420.0 1.9 add_convert_fusion.13
  421.9 0.1 conditional.11
  421.9 0.1 broadcast.680
  422.1 1.0 copy-done.4
  423.1 59.8 %all-reduce.16.cloned.1.call-done = bf16[2,128,2048]{2,1,0:T(8,128)(2,1)} async-done(((bf16[2,128,2048]{2,1,0:T(8,128)(2,1)}), bf16[2,128,2048]{2,1,0:T(8,128)(2,1)}) %all-reduce.16.cloned.1.call-update) | async-done | bytes 1048592 | tf_op jit(solution)/shard_map/psum | solution.py:111
  482.9 1.6 add_convert_fusion.12
  484.6 1.6 collective-permute-start.1
  486.2 6.8 conditional.12
  486.2 1.1 broadcast.683
  493.1 131.6 %all-reduce.18.cloned.1.call-done = bf16[2,128,2048]{2,1,0:T(8,128)(2,1)} async-done(((bf16[2,128,2048]{2,1,0:T(8,128)(2,1)}), bf16[2,128,2048]{2,1,0:T(8,128)(2,1)}) %all-reduce.18.cloned.1.call-update) | async-done | bytes 1048592 | tf_op jit(solution)/shard_map/psum | solution.py:109
  624.7 1.9 add_convert_fusion.11
  626.6 0.1 conditional.13
  626.8 1.0 copy-done.5
  627.8 61.5 %all-reduce.20.cloned.1.call-done = bf16[2,128,2048]{2,1,0:T(8,128)(2,1)} async-done(((bf16[2,128,2048]{2,1,0:T(8,128)(2,1)}), bf16[2,128,2048]{2,1,0:T(8,128)(2,1)}) %all-reduce.20.cloned.1.call-update) | async-done | bytes 1048592 | tf_op jit(solution)/shard_map/psum | solution.py:111
  689.3 1.6 add_convert_fusion.10
  690.9 1.6 collective-permute-start.2
  692.6 8.2 conditional.14
  692.6 1.1 broadcast.698
  700.8 117.7 %all-reduce.22.cloned.1.call-done = bf16[2,128,2048]{2,1,0:T(8,128)(2,1)} async-done(((bf16[2,128,2048]{2,1,0:T(8,128)(2,1)}), bf16[2,128,2048]{2,1,0:T(8,128)(2,1)}) %all-reduce.22.cloned.1.call-update) | async-done | bytes 1048592 | tf_op jit(solution)/shard_map/psum | solution.py:109
  818.5 1.9 add_convert_fusion.9
  820.4 0.1 conditional.15
  820.6 1.0 copy-done.6
  821.6 60.7 %all-reduce.24.cloned.1.call-done = bf16[2,128,2048]{2,1,0:T(8,128)(2,1)} async-done(((bf16[2,128,2048]{2,1,0:T(8,128)(2,1)}), bf16[2,128,2048]{2,1,0:T(8,128)(2,1)}) %all-reduce.24.cloned.1.call-update) | async-done | bytes 1048592 | tf_op jit(solution)/shard_map/psum | solution.py:111
  882.3 2.6 add_convert_fusion.8
  884.9 41.5 %copy.78 = bf16[2,128,16,32,64]{1,4,3,2,0:T(8,128)(2,1)} copy(bf16[2,128,16,32,64]{4,3,2,1,0:T(8,128)(2,1)} %get-tuple-element.229) | data formatting | bytes 33554432 | tf_op jit(solution)/shard_map/cond | solution.py:108
  926.4 41.4 %copy.79 = bf16[2,128,16,32,64]{1,4,3,2,0:T(8,128)(2,1)} copy(bf16[2,128,16,32,64]{4,3,2,1,0:T(8,128)(2,1)} %get-tuple-element.230) | data formatting | bytes 33554432 | tf_op jit(solution)/shard_map/cond | solution.py:108
  967.8 2.3 copy.193
  (49 shorter events, 1.0 us)
Async XLA Ops:
  7.2 221.1 %all-reduce.10.cloned.1.call-start = ((), (), s32[]{:S(2)}) async-start(), calls=%async_computation | async-start | bytes 2097152 | tf_op jit(solution)/shard_map/psum | solution.py:109
  53.2 46.0 %copy-start.8 = (bf16[1,2048]{1,0:T(2,128)(2,1)S(1)}, bf16[1,2048]{1,0:T(2,128)(2,1)}, u32[]{:S(2)}) copy-start(bf16[1,2048]{1,0:T(2,128)(2,1)} %param.33) | copy-start | bytes 12292
  53.2 46.1 %copy-start = (bf16[2,128,2048]{2,1,0:T(8,128)(2,1)S(1)}, bf16[2,128,2048]{2,1,0:T(8,128)(2,1)}, u32[]{:S(2)}) copy-start(bf16[2,128,2048]{2,1,0:T(8,128)(2,1)} %param.29) | copy-start | bytes 3145732
  53.2 46.1 %copy-start.7 = (s32[2,128]{1,0:T(2,128)S(1)}, s32[2,128]{1,0:T(2,128)}, u32[]{:S(2)}) copy-start(s32[2,128]{1,0:T(2,128)} %param.30) | copy-start | bytes 3076
  99.2 92.8 %copy-start.9 = (bf16[1,2048]{1,0:T(2,128)(2,1)S(1)}, bf16[1,2048]{1,0:T(2,128)(2,1)}, u32[]{:S(2)}) copy-start(bf16[1,2048]{1,0:T(2,128)(2,1)} %param.38) | copy-start | bytes 12292
  99.3 5.7 copy-start.1
  136.1 5.6 copy-start.2
  191.9 99.8 %all-reduce.12.cloned.1.call-start = ((), (), s32[]{:S(2)}) async-start(), calls=%async_computation.1 | async-start | bytes 2097152 | tf_op jit(solution)/shard_map/psum | solution.py:111
  257.5 1.0 copy-start.3
  258.5 161.5 %all-reduce.14.cloned.1.call-start = ((), (), s32[]{:S(2)}) async-start(), calls=%async_computation.2 | async-start | bytes 2097152 | tf_op jit(solution)/shard_map/psum | solution.py:109
  293.4 3.8 collective-permute-start
  303.9 179.0 %all-reduce.16.cloned.1.call-start = ((), (), s32[]{:S(2)}) async-start(), calls=%async_computation.3 | async-start | bytes 2097152 | tf_op jit(solution)/shard_map/psum | solution.py:111
  422.1 1.0 copy-start.4
  423.1 201.6 %all-reduce.18.cloned.1.call-start = ((), (), s32[]{:S(2)}) async-start(), calls=%async_computation.4 | async-start | bytes 2097152 | tf_op jit(solution)/shard_map/psum | solution.py:109
  484.6 1.6 collective-permute-start.1
  493.0 196.3 %all-reduce.20.cloned.1.call-start = ((), (), s32[]{:S(2)}) async-start(), calls=%async_computation.5 | async-start | bytes 2097152 | tf_op jit(solution)/shard_map/psum | solution.py:111
  626.8 1.0 copy-start.5
  627.8 190.7 %all-reduce.22.cloned.1.call-start = ((), (), s32[]{:S(2)}) async-start(), calls=%async_computation.6 | async-start | bytes 2097152 | tf_op jit(solution)/shard_map/psum | solution.py:109
  690.9 1.6 collective-permute-start.2
  700.8 181.5 %all-reduce.24.cloned.1.call-start = ((), (), s32[]{:S(2)}) async-start(), calls=%async_computation.7 | async-start | bytes 2097152 | tf_op jit(solution)/shard_map/psum | solution.py:111
  820.6 1.0 copy-start.6
  821.6 146.3 %all-reduce.26.cloned.1.call-start = ((), (), s32[]{:S(2)}) async-start(), calls=%async_computation.8 | async-start | bytes 2097152 | tf_op jit(solution)/shard_map/psum | solution.py:115
Sparse Core Ops, SparseCore 0:
  192.1 36.1 all-reduce.9
  258.6 33.1 all-reduce.11
  304.0 115.9 all-reduce.13
  423.2 59.7 all-reduce.15
  493.1 131.4 all-reduce.17
  627.9 61.3 all-reduce.19
  700.9 117.5 all-reduce.21
  821.7 60.5 all-reduce.23
  885.2 30.8 all-reduce.25
where the time goes:
time: 988 us; the launch traced here: 977 us
  waiting for transfers between devices  618 us (63%)
  local copies, waits for them, and re-layouts  197 us (20%)
  other arithmetic  78.3 us (8%)
  matrix products  43.7 us (4%)
  loops' own time  19.2 us (2%)
  between operations  14.2 us (1%)
    psum x4, waiting for transfers between devices, per_device(): attn_out = lax.psum(attn_partial, 'tp')  402 us
    psum x4, waiting for transfers between devices, per_device(): mlp_out = lax.psum(lax.cond(active, mlp_run, mlp_skip, mid_state), 'tp')  215 us
    unnamed x19, local copies, waits for them, and re-layouts  98.1 us
    cond x2, local copies, waits for them, and re-layouts, per_device(): lax.cond(active, attn_run, attn_skip, (state_h, key_local, value_local))  82.9 us
    cond x3, other arithmetic  59.9 us
  transfers between devices with their start and end apart: 12, of which 9 were waited for; matrix products, arithmetic and copies ran while one was open for 8% of the time, Pallas kernels for 0%

commit v1 on v0

v1 whole, which is shorter than its diff:
```python
import functools
import math
import jax
import jax.numpy as jnp
from jax import lax
from jax.experimental import pallas as pl
from jax.experimental.pallas import tpu as pltpu
from jax.sharding import PartitionSpec as P

ROPE_THETA = 500000.0
SCALE_FACTOR = 8.0
LOW_FACTOR = 1.0
HIGH_FACTOR = 4.0
ORIG_CONTEXT = 8192.0
NORM_EPS = 1e-5
MESH = pl.DeviceIdType.MESH
F32 = jnp.float32
BF16 = jnp.bfloat16

COLS = 512
ROWS = 1024
KV_SLOTS = 4
NORM_ROWS = 16


def rope_freqs(head_dim):
    freq_index = jnp.arange(head_dim // 2, dtype=jnp.float32)
    base_freq = ROPE_THETA ** (-2.0 * freq_index / head_dim)
    wave_len = 2.0 * math.pi / base_freq
    smooth_t = (ORIG_CONTEXT / wave_len - LOW_FACTOR) / (HIGH_FACTOR - LOW_FACTOR)
    mixed_freq = (1.0 - smooth_t) * base_freq / SCALE_FACTOR + smooth_t * base_freq
    long_freq = jnp.where(wave_len > ORIG_CONTEXT / LOW_FACTOR, base_freq / SCALE_FACTOR, mixed_freq)
    return jnp.where(wave_len < ORIG_CONTEXT / HIGH_FACTOR, base_freq, long_freq)


def layer_kernel(dims, cos_ref, sin_ref, pos_ref, ga_ref, gm_ref, hid, kc, vc, wq, wk, wv, wo, wg, wu, wd,
                 hout, knew, vnew,
                 wqkv_v, wo_v, wg_v, wu_v, wd_v, k_v, v_v, hbuf, recvp, recvd, nbuf, qt, ubuf, sc,
                 hid_sem, wqkv_sem, wo_sem, gu_sem, wd_sem, k_sem, v_sem,
                 p_send, p_recv, d_send, d_recv, h_send, h_recv):
    n_groups, n_batch, d_model, heads, seq, hd, ff, n_pp, n_tp = dims
    hw = heads * hd
    n_chunk = d_model // COLS
    n_gu = ff // COLS
    n_kb = ff // ROWS
    pp = lax.axis_index("pp")
    tp = lax.axis_index("tp")
    peer = {"tp": lax.rem(tp + 1, n_tp)}
    nxt = {"pp": lax.rem(pp + 1, n_pp)}
    prv = {"pp": lax.rem(pp + n_pp - 1, n_pp)}

    def kv_copies(item, slot):
        g = item // heads
        h = lax.rem(item, heads)
        return (pltpu.make_async_copy(kc.at[g, h], k_v.at[slot], k_sem.at[slot]),
                pltpu.make_async_copy(vc.at[g, h], v_v.at[slot], v_sem.at[slot]))

    def gu_copies(j):
        cols = pl.ds(j * COLS, COLS)
        return (pltpu.make_async_copy(wg.at[:, cols], wg_v.at[j], gu_sem.at[0, j]),
                pltpu.make_async_copy(wu.at[:, cols], wu_v.at[j], gu_sem.at[1, j]))

    def wd_copy(nb, kb):
        return pltpu.make_async_copy(wd.at[pl.ds(kb * ROWS, ROWS), pl.ds(nb * COLS, COLS)], wd_v.at[kb], wd_sem.at[kb])

    def qkv_copies():
        return [pltpu.make_async_copy(src, wqkv_v.at[i], wqkv_sem.at[i]) for i, src in enumerate((wq, wk, wv))]

    def wo_copy():
        return pltpu.make_async_copy(wo, wo_v, wo_sem)

    def hid_copy(g):
        return pltpu.make_async_copy(hid.at[g], hbuf.at[g], hid_sem.at[g])

    def piece(ref, g, c):
        return ref.at[g, :, pl.ds(pl.multiple_of(c * COLS, COLS), COLS)]

    def p_copy(g, c):
        return pltpu.make_async_remote_copy(piece(hout, g, c), piece(recvp, g, c), p_send.at[g, c], p_recv.at[g, c], device_id=peer, device_id_type=MESH)

    def d_copy(g, c):
        return pltpu.make_async_remote_copy(piece(recvp, g, c), piece(recvd, g, c), d_send.at[g, c], d_recv.at[g, c], device_id=peer, device_id_type=MESH)

    def h_copy(g, c):
        return pltpu.make_async_remote_copy(piece(hout, g, c), piece(hbuf, g, c), h_send.at[g, c], h_recv.at[g, c], device_id=nxt, device_id_type=MESH)

    first = pp == 0
    last = pp == n_pp - 1

    @pl.when(first)
    def _():
        for g in range(n_groups):
            hid_copy(g).start()
    for copy in qkv_copies():
        copy.start()
    for slot in range(KV_SLOTS):
        for copy in kv_copies(slot, slot):
            copy.start()
    wo_copy().start()

    barrier = pltpu.get_barrier_semaphore()
    for other in (peer, nxt, prv):
        pl.semaphore_signal(barrier, inc=1, device_id=other, device_id_type=MESH)
    pl.semaphore_wait(barrier, 3)

    for copy in qkv_copies():
        copy.wait()
    for j in range(n_gu):
        for copy in gu_copies(j):
            copy.start()
    for kb in range(n_kb):
        wd_copy(0, kb).start()

    def norm_rows(g, gain_ref, with_partial):
        def body(r, carry):
            rows = pl.ds(pl.multiple_of(r * NORM_ROWS, NORM_ROWS), NORM_ROWS)
            x = hbuf[g, rows, :].astype(F32)
            if with_partial:
                part = (hout[g, rows, :].astype(F32) + recvp[g, rows, :].astype(F32)).astype(BF16)
                x = (x + part.astype(F32)).astype(BF16)
                hbuf[g, rows, :] = x
                x = x.astype(F32)
            inv = lax.rsqrt(jnp.mean(x * x, axis=-1, keepdims=True) + NORM_EPS)
            nbuf[rows, :] = (x * inv * gain_ref[...].astype(F32)).astype(BF16)
            return carry
        lax.fori_loop(0, n_batch // NORM_ROWS, body, 0)

    def attention_phase(g, carry):
        @pl.when(first)
        def _():
            hid_copy(g).wait()

        @pl.when(pp > 0)
        def _():
            for c in range(n_chunk):
                h_copy(g, c).wait_recv()

        norm_rows(g, ga_ref, False)
        cosine = cos_ref[g]
        sine = sin_ref[g]
        half = hd // 2
        for which in range(3):
            for c in range(hw // COLS):
                cols = slice(c * COLS, (c + 1) * COLS)
                prod = jnp.dot(nbuf[...], wqkv_v[which, :, cols], preferred_element_type=F32)
                prod_t = prod.T
                for h in range(COLS // hd):
                    head = c * (COLS // hd) + h
                    a = prod_t[h * hd:h * hd + half]
                    b = prod_t[h * hd + half:(h + 1) * hd]
                    if which < 2:
                        a, b = a * cosine - b * sine, b * cosine + a * sine
                    a, b = a.astype(BF16), b.astype(BF16)
                    if which == 0:
                        qt[head * hd:head * hd + half, :] = a
                        qt[head * hd + half:(head + 1) * hd, :] = b
                    else:
                        dst = knew if which == 1 else vnew
                        dst[g, head, 0:half, :] = a
                        dst[g, head, half:hd, :] = b

        pos = pos_ref[g]
        row_id = lax.broadcasted_iota(jnp.int32, (seq, n_batch), 0)
        hit = row_id == pos
        seen = row_id <= pos

        def head_body(h, inner):
            item = g * heads + h
            slot = lax.rem(item, KV_SLOTS)
            for copy in kv_copies(item, slot):
                copy.wait()
            rows = pl.ds(pl.multiple_of(h * hd, hd), hd)
            q = qt[rows, :].astype(F32)
            fresh = jnp.sum(q * knew[g, h].astype(F32), axis=0, keepdims=True)
            for s in range(seq):
                sc[s:s + 1, :] = jnp.sum(k_v[slot, s].astype(F32) * q, axis=0, keepdims=True)
            scores = jnp.where(hit, fresh, sc[...]) * hd ** -0.5
            scores = jnp.where(seen, scores, -jnp.inf)
            top = jnp.max(scores, axis=0, keepdims=True)
            expd = jnp.exp(scores - top)
            probs = (expd / jnp.sum(expd, axis=0, keepdims=True)).astype(BF16).astype(F32)
            sc[...] = jnp.where(hit, 0.0, probs)
            acc = jnp.sum(jnp.where(hit, probs, 0.0), axis=0, keepdims=True) * vnew[g, h].astype(F32)
            for s in range(seq):
                acc = acc + sc[s:s + 1, :] * v_v[slot, s].astype(F32)
            qt[rows, :] = acc.astype(BF16)

            @pl.when(item + KV_SLOTS < n_groups * heads)
            def _():
                for copy in kv_copies(item + KV_SLOTS, slot):
                    copy.start()
            return inner
        lax.fori_loop(0, heads, head_body, 0)

        @pl.when(g == 0)
        def _():
            wo_copy().wait()
        for c in range(hw // COLS):
            cols = slice(c * COLS, (c + 1) * COLS)
            nbuf[:, cols] = qt[cols, :].astype(F32).T.astype(BF16)

        for c in range(n_chunk):
            part = jnp.dot(nbuf[:, 0:hw], wo_v[:, c * COLS:(c + 1) * COLS], preferred_element_type=F32)
            hout[g, :, c * COLS:(c + 1) * COLS] = part.astype(BF16)
            p_copy(g, c).start()
        return carry

    def mlp_phase(g, carry):
        for c in range(n_chunk):
            p_copy(g, c).wait()
        norm_rows(g, gm_ref, True)

        def gu_body(j, inner):
            @pl.when(g == 0)
            def _():
                for copy in gu_copies(j):
                    copy.wait()
            gate = jnp.dot(nbuf[...], wg_v[j], preferred_element_type=F32)
            up = jnp.dot(nbuf[...], wu_v[j], preferred_element_type=F32)
            ubuf[:, pl.ds(pl.multiple_of(j * COLS, COLS), COLS)] = (jax.nn.silu(gate) * up).astype(BF16)
            return inner
        lax.fori_loop(0, n_gu, gu_body, 0)

        def wd_body(nb, inner):
            acc = None
            for kb in range(n_kb):
                wd_copy(nb, kb).wait()
                prod = jnp.dot(ubuf[:, kb * ROWS:(kb + 1) * ROWS], wd_v[kb], preferred_element_type=F32)
                acc = prod if acc is None else acc + prod

                @pl.when(g * n_chunk + nb + 1 < n_groups * n_chunk)
                def _():
                    wd_copy(lax.rem(nb + 1, n_chunk), kb).start()
            recvp[g, :, pl.ds(pl.multiple_of(nb * COLS, COLS), COLS)] = acc.astype(BF16)
            d_copy(g, nb).start()
            return inner
        lax.fori_loop(0, n_chunk, wd_body, 0)
        return carry

    def finish_phase(g, carry):
        for c in range(n_chunk):
            d_copy(g, c).wait()
            cols = slice(c * COLS, (c + 1) * COLS)
            part = (recvd[g, :, cols].astype(F32) + recvp[g, :, cols].astype(F32)).astype(BF16)
            hout[g, :, cols] = (hbuf[g, :, cols].astype(F32) + part.astype(F32)).astype(BF16)

            @pl.when(jnp.logical_not(last))
            def _():
                h_copy(g, c).start()
        return carry

    lax.fori_loop(0, n_groups, attention_phase, 0)
    lax.fori_loop(0, n_groups, mlp_phase, 0)
    lax.fori_loop(0, n_groups, finish_phase, 0)

    @pl.when(jnp.logical_not(last))
    def _():
        for g in range(n_groups):
            for c in range(n_chunk):
                h_copy(g, c).wait_send()


def run_layer(dims, *args):
    n_groups, n_batch, d_model, heads, seq, hd, ff, n_pp, n_tp = dims
    hw = heads * hd
    n_chunk = d_model // COLS
    n_gu = ff // COLS
    n_kb = ff // ROWS
    vmem = pl.BlockSpec(memory_space=pltpu.VMEM)
    hbm = pl.BlockSpec(memory_space=pl.ANY)
    dma = pltpu.SemaphoreType.DMA
    return pl.pallas_call(
        functools.partial(layer_kernel, dims),
        out_shape=(jax.ShapeDtypeStruct((n_groups, n_batch, d_model), BF16),
                   jax.ShapeDtypeStruct((n_groups, heads, hd, n_batch), BF16),
                   jax.ShapeDtypeStruct((n_groups, heads, hd, n_batch), BF16)),
        in_specs=[vmem] * 5 + [hbm] * 10,
        out_specs=(vmem, vmem, vmem),
        scratch_shapes=[
            pltpu.VMEM((3, d_model, hw), BF16),
            pltpu.VMEM((hw, d_model), BF16),
            pltpu.VMEM((n_gu, d_model, COLS), BF16),
            pltpu.VMEM((n_gu, d_model, COLS), BF16),
            pltpu.VMEM((n_kb, ROWS, COLS), BF16),
            pltpu.VMEM((KV_SLOTS, seq, hd, n_batch), BF16),
            pltpu.VMEM((KV_SLOTS, seq, hd, n_batch), BF16),
            pltpu.VMEM((n_groups, n_batch, d_model), BF16),
            pltpu.VMEM((n_groups, n_batch, d_model), BF16),
            pltpu.VMEM((n_groups, n_batch, d_model), BF16),
            pltpu.VMEM((n_batch, d_model), BF16),
            pltpu.VMEM((hw, n_batch), BF16),
            pltpu.VMEM((n_batch, ff), BF16),
            pltpu.VMEM((seq, n_batch), F32),
            dma((n_groups,)), dma((3,)), dma, dma((2, n_gu)), dma((n_kb,)), dma((KV_SLOTS,)), dma((KV_SLOTS,)),
            dma((n_groups, n_chunk)), dma((n_groups, n_chunk)), dma((n_groups, n_chunk)),
            dma((n_groups, n_chunk)), dma((n_groups, n_chunk)), dma((n_groups, n_chunk)),
        ],
        compiler_params=pltpu.CompilerParams(collective_id=0, has_side_effects=True, vmem_limit_bytes=67043328),
        name="layer",
    )(*args)


def solution(mesh):
    n_pp = mesh.shape["pp"]
    n_tp = mesh.shape["tp"]
    cache_spec = P("pp", "dp", None, "tp", None, None)
    col_spec = P("pp", None, "tp")
    row_spec = P("pp", "tp", None)
    gain_spec = P("pp", None)
    in_specs = (P("dp", None, None), P("dp", None), cache_spec, cache_spec, gain_spec, col_spec, col_spec, col_spec, row_spec, gain_spec, col_spec, col_spec, row_spec)
    out_specs = (P("dp", None, None), cache_spec, cache_spec)

    def per_device(hidden, positions, key_cache, value_cache, attn_norm, w_query, w_key, w_value, w_out, mlp_norm, w_gate, w_up, w_down):
        _, n_groups, n_batch, heads, seq, hd = key_cache.shape
        d_model = hidden.shape[-1]
        ff = w_gate.shape[-1]
        dims = (n_groups, n_batch, d_model, heads, seq, hd, ff, n_pp, n_tp)
        angles = positions.astype(F32)[:, None, :] * rope_freqs(hd)[None, :, None]
        key_t = jnp.transpose(key_cache[0], (0, 2, 3, 4, 1))
        value_t = jnp.transpose(value_cache[0], (0, 2, 3, 4, 1))
        state, key_new, value_new = run_layer(
            dims, jnp.cos(angles), jnp.sin(angles), positions[:, None, :], attn_norm, mlp_norm, hidden, key_t, value_t,
            w_query[0], w_key[0], w_value[0], w_out[0], w_gate[0], w_up[0], w_down[0])

        stage = lax.axis_index("pp")
        from_last = [lax.ppermute(state, "pp", [(n_pp - 1, dst)]) for dst in range(1, n_pp - 1)]
        from_last.append(lax.ppermute(from_last[0], "pp", [(1, 0)]))
        final = jnp.where(stage == n_pp - 1, state, sum(from_last[1:], from_last[0]))

        row_hit = jnp.arange(seq, dtype=jnp.int32)[None, None, :, None, None] == positions[:, None, None, None, :]
        key_t = jnp.where(row_hit, key_new[:, :, None], key_t)
        value_t = jnp.where(row_hit, value_new[:, :, None], value_t)
        return final, jnp.transpose(key_t, (0, 4, 1, 2, 3))[None], jnp.transpose(value_t, (0, 4, 1, 2, 3))[None]

    return jax.shard_map(per_device, mesh=mesh, in_specs=in_specs, out_specs=out_specs, check_vma=False)
```

time: 988 us -> 259 us (0.26)
  the two profiles are of different devices: /device:TPU:0 before, /device:TPU:1 now
where the time goes in v1:
time: 259 us; the launch traced here: 258 us
  Pallas kernels  121 us (47%)
  waiting for transfers between devices  105 us (41%)
  other arithmetic  27.6 us (11%)
  starting transfers between devices  4.35 us (2%)
    pallas_call x1, Pallas kernels, run_layer(): pl.pallas_call(functools.partial(layer_kernel, dims), out_shape=(jax.Shap...  121 us
    ppermute x2, waiting for transfers between devices, per_device(): lax.ppermute(state, 'pp', [(n_pp - 1, dst)])  105 us
    select_n x1, other arithmetic, per_device(): value_t = jnp.where(row_hit, value_new[:, :, None], value_t)  23 us
  transfers between devices with their start and end apart: 3, of which 1 were waited for; matrix products, arithmetic and copies ran while one was open for 9% of the time, Pallas kernels for 0%

profile of v1, /device:TPU:1, one launch (start us, length us, event | category | flops | bytes accessed | tf_op | source)
XLA Modules:
  0.0 258.2 jit_solution(16980234720175461290)
XLA Ops:
  0.7 0.7 convert_element_type.3
  1.3 0.8 multiply_sine_fusion
  2.2 120.6 %layer.1 = (bf16[2,128,2048]{2,1,0:T(8,128)(2,1)}, bf16[2,16,64,128]{3,2,1,0:T(8,128)(2,1)}, bf16[2,16,64,128]{3,2,1,0:T(8,128)(2,1)}) custom-call(f32[2,32,128]{2,1,0:T(8,128)} %get-tuple-element.12.cos_ref, f32[2,32,128]{2,1,0:T(8,128)} %get-tuple-element.11.sin_ref, s32[2,1,128]{2,1,0:T(1,128)} %bitcast.27, bf16[1,2048]{1,0:T(2,128)(2,1)} %ga_ref.1, ...), custom_call_target="tpu_custom_call" | custom-call | tf_op jit(solution)/shard_map/layer/pallas_call | solution.py:272
  122.8 1.3 collective-permute-start
  124.1 0.7 collective-permute-start.1
  124.8 0.7 iota_compare_fusion
  125.5 105.0 %collective-permute-done = bf16[2,128,2048]{2,1,0:T(8,128)(2,1)S(1)} collective-permute-done((bf16[2,128,2048]{2,1,0:T(8,128)(2,1)}, bf16[2,128,2048]{2,1,0:T(8,128)(2,1)S(1)}, u32[]{:S(2)}, u32[]{:S(2)}) %collective-permute-start) | collective-permute-done | bytes 1048608 | tf_op jit(solution)/shard_map/ppermute | solution.py:326
  230.5 2.3 collective-permute-start.2
  232.8 0.0 copy-start
  232.8 23.0 %broadcast_select_fusion = (bf16[1,2,128,16,32,64]{2,5,4,3,1,0:T(8,128)(2,1)}, bf16[1,2,128,16,32,64]{2,5,4,3,1,0:T(8,128)(2,1)}) fusion(bf16[1,2,128,16,32,64]{2,5,4,3,1,0:T(8,128)(2,1)} %param.16, pred[2,128,32]{1,2,0:T(8,128)(4,1)S(1)} %iota_compare_fusion, bf16[2,128,16,64]{1,3,2,0:T(8,128)(2,1)} %bitcast.26, bf16[1,2,128,16,32,64]{2,5,4,3,1,0:T(8,128)(2,1)} %param.15, ...), kind=kLoop, calls=%fused_computation | loop fusion | flops 16777216 | bytes 68165632 | tf_op jit(solution)/shard_map/jit(_where)/select_n | solution.py:332
  255.8 0.0 collective-permute-done.1
  255.8 0.0 collective-permute-done.2
  255.8 0.0 copy-done
  255.8 2.4 add_select_fusion
  (1 shorter events, 0.0 us)
Async XLA Ops:
  122.8 107.7 %collective-permute-start = (bf16[2,128,2048]{2,1,0:T(8,128)(2,1)}, bf16[2,128,2048]{2,1,0:T(8,128)(2,1)S(1)}, u32[]{:S(2)}, u32[]{:S(2)}) collective-permute-start(bf16[2,128,2048]{2,1,0:T(8,128)(2,1)} %get-tuple-element.6), channel_id=1, source_target_pairs={{3,1},{7,5}} | collective-permute-start | bytes 3145736 | tf_op jit(solution)/shard_map/ppermute | solution.py:326
  124.1 131.7 %collective-permute-start.1 = (bf16[2,128,2048]{2,1,0:T(8,128)(2,1)}, bf16[2,128,2048]{2,1,0:T(8,128)(2,1)S(1)}, u32[]{:S(2)}, u32[]{:S(2)}) collective-permute-start(bf16[2,128,2048]{2,1,0:T(8,128)(2,1)} %get-tuple-element.6), channel_id=1, source_target_pairs={{3,2},{7,6}} | collective-permute-start | bytes 3145736 | tf_op jit(solution)/shard_map/ppermute | solution.py:326
  230.5 25.3 %collective-permute-start.2 = (bf16[2,128,2048]{2,1,0:T(8,128)(2,1)S(1)}, bf16[2,128,2048]{2,1,0:T(8,128)(2,1)}, u32[]{:S(2)}, u32[]{:S(2)}) collective-permute-start(bf16[2,128,2048]{2,1,0:T(8,128)(2,1)S(1)} %collective-permute-done), channel_id=1, source_target_pairs={{1,0},{5,4}} | collective-permute-start | bytes 3145736 | tf_op jit(solution)/shard_map/ppermute | solution.py:327
  232.8 23.0 %copy-start = (bf16[2,128,2048]{2,1,0:T(8,128)(2,1)S(1)}, bf16[2,128,2048]{2,1,0:T(8,128)(2,1)}, u32[]{:S(2)}) copy-start(bf16[2,128,2048]{2,1,0:T(8,128)(2,1)} %get-tuple-element.6) | copy-start | bytes 3145732

commit v2 on v1

--- a/solution.py
+++ b/solution.py
@@ -19,8 +19,8 @@
 
 COLS = 512
 ROWS = 1024
-KV_SLOTS = 4
-NORM_ROWS = 16
+SLOTS = 8
+NORM_ROWS = 32
 
 
 def rope_freqs(head_dim):
@@ -35,8 +35,8 @@
 
 def layer_kernel(dims, cos_ref, sin_ref, pos_ref, ga_ref, gm_ref, hid, kc, vc, wq, wk, wv, wo, wg, wu, wd,
                  hout, knew, vnew,
-                 wqkv_v, wo_v, wg_v, wu_v, wd_v, k_v, v_v, hbuf, recvp, recvd, nbuf, qt, ubuf, sc,
-                 hid_sem, wqkv_sem, wo_sem, gu_sem, wd_sem, k_sem, v_sem,
+                 wqkv_v, wo_v, wg_v, wu_v, ring, hbuf, recvp, recvd, nbuf, qt, ubuf, sc,
+                 hid_sem, wqkv_sem, wo_sem, gu_sem, ring_sem,
                  p_send, p_recv, d_send, d_recv, h_send, h_recv):
     n_groups, n_batch, d_model, heads, seq, hd, ff, n_pp, n_tp = dims
     hw = heads * hd
@@ -49,19 +49,30 @@
     nxt = {"pp": lax.rem(pp + 1, n_pp)}
     prv = {"pp": lax.rem(pp + n_pp - 1, n_pp)}
 
+    n_kv = n_groups * heads
+    n_wd = n_chunk * n_kb
+    n_items = n_kv + n_groups * n_wd
+    slabs = COLS // n_batch
+    deep = ROWS // hd
+
     def kv_copies(item, slot):
         g = item // heads
         h = lax.rem(item, heads)
-        return (pltpu.make_async_copy(kc.at[g, h], k_v.at[slot], k_sem.at[slot]),
-                pltpu.make_async_copy(vc.at[g, h], v_v.at[slot], v_sem.at[slot]))
+        return (pltpu.make_async_copy(kc.at[g, h], ring.at[slot, pl.ds(0, seq)], ring_sem.at[slot, 0]),
+                pltpu.make_async_copy(vc.at[g, h], ring.at[slot, pl.ds(seq, seq)], ring_sem.at[slot, 1]))
+
+    def wd_copies(item, slot):
+        tile = lax.rem(item - n_kv, n_wd)
+        nb = tile // n_kb
+        kb = lax.rem(tile, n_kb)
+        return [pltpu.make_async_copy(
+            wd.at[pl.ds(kb * deep, deep), :, pl.ds(pl.multiple_of(nb * COLS + i * n_batch, n_batch), n_batch)],
+            ring.at[slot, pl.ds(i * deep, deep)], ring_sem.at[slot, i]) for i in range(slabs)]
 
     def gu_copies(j):
         cols = pl.ds(j * COLS, COLS)
         return (pltpu.make_async_copy(wg.at[:, cols], wg_v.at[j], gu_sem.at[0, j]),
                 pltpu.make_async_copy(wu.at[:, cols], wu_v.at[j], gu_sem.at[1, j]))
-
-    def wd_copy(nb, kb):
-        return pltpu.make_async_copy(wd.at[pl.ds(kb * ROWS, ROWS), pl.ds(nb * COLS, COLS)], wd_v.at[kb], wd_sem.at[kb])
 
     def qkv_copies():
         return [pltpu.make_async_copy(src, wqkv_v.at[i], wqkv_sem.at[i]) for i, src in enumerate((wq, wk, wv))]
@@ -93,7 +104,7 @@
             hid_copy(g).start()
     for copy in qkv_copies():
         copy.start()
-    for slot in range(KV_SLOTS):
+    for slot in range(SLOTS):
         for copy in kv_copies(slot, slot):
             copy.start()
     wo_copy().start()
@@ -108,9 +119,6 @@
     for j in range(n_gu):
         for copy in gu_copies(j):
             copy.start()
-    for kb in range(n_kb):
-        wd_copy(0, kb).start()
-
     def norm_rows(g, gain_ref, with_partial):
         def body(r, carry):
             rows = pl.ds(pl.multiple_of(r * NORM_ROWS, NORM_ROWS), NORM_ROWS)
@@ -166,14 +174,14 @@
 
         def head_body(h, inner):
             item = g * heads + h
-            slot = lax.rem(item, KV_SLOTS)
+            slot = lax.rem(item, SLOTS)
             for copy in kv_copies(item, slot):
                 copy.wait()
             rows = pl.ds(pl.multiple_of(h * hd, hd), hd)
             q = qt[rows, :].astype(F32)
             fresh = jnp.sum(q * knew[g, h].astype(F32), axis=0, keepdims=True)
             for s in range(seq):
-                sc[s:s + 1, :] = jnp.sum(k_v[slot, s].astype(F32) * q, axis=0, keepdims=True)
+                sc[s:s + 1, :] = jnp.sum(ring[slot, s].astype(F32) * q, axis=0, keepdims=True)
             scores = jnp.where(hit, fresh, sc[...]) * hd ** -0.5
             scores = jnp.where(seen, scores, -jnp.inf)
             top = jnp.max(scores, axis=0, keepdims=True)
@@ -182,12 +190,17 @@
             sc[...] = jnp.where(hit, 0.0, probs)
             acc = jnp.sum(jnp.where(hit, probs, 0.0), axis=0, keepdims=True) * vnew[g, h].astype(F32)
             for s in range(seq):
-                acc = acc + sc[s:s + 1, :] * v_v[slot, s].astype(F32)
+                acc = acc + sc[s:s + 1, :] * ring[slot, seq + s].astype(F32)
             qt[rows, :] = acc.astype(BF16)
 
-            @pl.when(item + KV_SLOTS < n_groups * heads)
-            def _():
-                for copy in kv_copies(item + KV_SLOTS, slot):
+            @pl.when(item + SLOTS < n_kv)
+            def _():
+                for copy in kv_copies(item + SLOTS, slot):
+                    copy.start()
+
+            @pl.when(item + SLOTS >= n_kv)
+            def _():
+                for copy in wd_copies(item + SLOTS, slot):
                     copy.start()
             return inner
         lax.fori_loop(0, heads, head_body, 0)
@@ -202,6 +215,7 @@
         for c in range(n_chunk):
             part = jnp.dot(nbuf[:, 0:hw], wo_v[:, c * COLS:(c + 1) * COLS], preferred_element_type=F32)
             hout[g, :, c * COLS:(c + 1) * COLS] = part.astype(BF16)
+        for c in range(n_chunk):
             p_copy(g, c).start()
         return carry
 
@@ -210,48 +224,64 @@
             p_copy(g, c).wait()
         norm_rows(g, gm_ref, True)
 
-        def gu_body(j, inner):
+        pair = n_gu // n_chunk
+
+        def gu_body(c, inner):
+            tiles = [c * pair + i for i in range(pair)]
+
             @pl.when(g == 0)
             def _():
-                for copy in gu_copies(j):
+                for j in tiles:
+                    for copy in gu_copies(j):
+                        copy.wait()
+
+            @pl.when(g > 0)
+            def _():
+                finish_piece(g - 1, c)
+            for j in tiles:
+                gate = jnp.dot(nbuf[...], wg_v[j], preferred_element_type=F32)
+                up = jnp.dot(nbuf[...], wu_v[j], preferred_element_type=F32)
+                ubuf[:, pl.ds(pl.multiple_of(j * COLS, COLS), COLS)] = (jax.nn.silu(gate) * up).astype(BF16)
+            return inner
+        lax.fori_loop(0, n_chunk, gu_body, 0)
+
+        def wd_body(nb, inner):
+            item = n_kv + g * n_wd + nb * n_kb
+            slot = lax.rem(item, SLOTS)
+            for kb in range(n_kb):
+                for copy in wd_copies(item + kb, slot + kb):
                     copy.wait()
-            gate = jnp.dot(nbuf[...], wg_v[j], preferred_element_type=F32)
-            up = jnp.dot(nbuf[...], wu_v[j], preferred_element_type=F32)
-            ubuf[:, pl.ds(pl.multiple_of(j * COLS, COLS), COLS)] = (jax.nn.silu(gate) * up).astype(BF16)
-            return inner
-        lax.fori_loop(0, n_gu, gu_body, 0)
-
-        def wd_body(nb, inner):
             acc = None
             for kb in range(n_kb):
-                wd_copy(nb, kb).wait()
-                prod = jnp.dot(ubuf[:, kb * ROWS:(kb + 1) * ROWS], wd_v[kb], preferred_element_type=F32)
+                tile = jnp.concatenate([ring[slot + kb, i * deep:(i + 1) * deep].reshape(ROWS, n_batch) for i in range(slabs)], axis=1)
+                prod = jnp.dot(ubuf[:, kb * ROWS:(kb + 1) * ROWS], tile, preferred_element_type=F32)
                 acc = prod if acc is None else acc + prod
-
-                @pl.when(g * n_chunk + nb + 1 < n_groups * n_chunk)
-                def _():
-                    wd_copy(lax.rem(nb + 1, n_chunk), kb).start()
             recvp[g, :, pl.ds(pl.multiple_of(nb * COLS, COLS), COLS)] = acc.astype(BF16)
             d_copy(g, nb).start()
+
+            @pl.when(item + SLOTS < n_items)
+            def _():
+                for kb in range(n_kb):
+                    for copy in wd_copies(item + SLOTS + kb, slot + kb):
+                        copy.start()
             return inner
         lax.fori_loop(0, n_chunk, wd_body, 0)
         return carry
 
-    def finish_phase(g, carry):
-        for c in range(n_chunk):
-            d_copy(g, c).wait()
-            cols = slice(c * COLS, (c + 1) * COLS)
-            part = (recvd[g, :, cols].astype(F32) + recvp[g, :, cols].astype(F32)).astype(BF16)
-            hout[g, :, cols] = (hbuf[g, :, cols].astype(F32) + part.astype(F32)).astype(BF16)
-
-            @pl.when(jnp.logical_not(last))
-            def _():
-                h_copy(g, c).start()
-        return carry
+    def finish_piece(g, c):
+        d_copy(g, c).wait()
+        cols = pl.ds(pl.multiple_of(c * COLS, COLS), COLS)
+        part = (recvd[g, :, cols].astype(F32) + recvp[g, :, cols].astype(F32)).astype(BF16)
+        hout[g, :, cols] = (hbuf[g, :, cols].astype(F32) + part.astype(F32)).astype(BF16)
+
+        @pl.when(jnp.logical_not(last))
+        def _():
+            h_copy(g, c).start()
 
     lax.fori_loop(0, n_groups, attention_phase, 0)
     lax.fori_loop(0, n_groups, mlp_phase, 0)
-    lax.fori_loop(0, n_groups, finish_phase, 0)
+    for c in range(n_chunk):
+        finish_piece(n_groups - 1, c)
 
     @pl.when(jnp.logical_not(last))
     def _():
@@ -265,7 +295,7 @@
     hw = heads * hd
     n_chunk = d_model // COLS
     n_gu = ff // COLS
-    n_kb = ff // ROWS
+    assert ROWS * COLS == 2 * seq * hd * n_batch and SLOTS % (ff // ROWS) == 0
     vmem = pl.BlockSpec(memory_space=pltpu.VMEM)
     hbm = pl.BlockSpec(memory_space=pl.ANY)
     dma = pltpu.SemaphoreType.DMA
@@ -281,9 +311,7 @@
             pltpu.VMEM((hw, d_model), BF16),
             pltpu.VMEM((n_gu, d_model, COLS), BF16),
             pltpu.VMEM((n_gu, d_model, COLS), BF16),
-            pltpu.VMEM((n_kb, ROWS, COLS), BF16),
-            pltpu.VMEM((KV_SLOTS, seq, hd, n_batch), BF16),
-            pltpu.VMEM((KV_SLOTS, seq, hd, n_batch), BF16),
+            pltpu.VMEM((SLOTS, 2 * seq, hd, n_batch), BF16),
             pltpu.VMEM((n_groups, n_batch, d_model), BF16),
             pltpu.VMEM((n_groups, n_batch, d_model), BF16),
             pltpu.VMEM((n_groups, n_batch, d_model), BF16),
@@ -291,7 +319,7 @@
             pltpu.VMEM((hw, n_batch), BF16),
             pltpu.VMEM((n_batch, ff), BF16),
             pltpu.VMEM((seq, n_batch), F32),
-            dma((n_groups,)), dma((3,)), dma, dma((2, n_gu)), dma((n_kb,)), dma((KV_SLOTS,)), dma((KV_SLOTS,)),
+            dma((n_groups,)), dma((3,)), dma, dma((2, n_gu)), dma((SLOTS, COLS // n_batch)),
             dma((n_groups, n_chunk)), dma((n_groups, n_chunk)), dma((n_groups, n_chunk)),
             dma((n_groups, n_chunk)), dma((n_groups, n_chunk)), dma((n_groups, n_chunk)),
         ],
@@ -320,11 +348,10 @@
         value_t = jnp.transpose(value_cache[0], (0, 2, 3, 4, 1))
         state, key_new, value_new = run_layer(
             dims, jnp.cos(angles), jnp.sin(angles), positions[:, None, :], attn_norm, mlp_norm, hidden, key_t, value_t,
-            w_query[0], w_key[0], w_value[0], w_out[0], w_gate[0], w_up[0], w_down[0])
+            w_query[0], w_key[0], w_value[0], w_out[0], w_gate[0], w_up[0], w_down[0].reshape(ff // hd, hd, d_model))
 
         stage = lax.axis_index("pp")
-        from_last = [lax.ppermute(state, "pp", [(n_pp - 1, dst)]) for dst in range(1, n_pp - 1)]
-        from_last.append(lax.ppermute(from_last[0], "pp", [(1, 0)]))
+        from_last = [lax.ppermute(state, "pp", [(n_pp - 1, dst)]) for dst in range(n_pp - 1)]
         final = jnp.where(stage == n_pp - 1, state, sum(from_last[1:], from_last[0]))
 
         row_hit = jnp.arange(seq, dtype=jnp.int32)[None, None, :, None, None] == positions[:, None, None, None, :]

time: 259 us -> 202 us (0.78)
  the two profiles are of different devices: /device:TPU:1 before, /device:TPU:0 now
where the time goes in v2:
time: 202 us; the launch traced here: 201 us
  waiting for transfers between devices  108 us (53%)
  Pallas kernels  62.6 us (31%)
  other arithmetic  27.6 us (14%)
  starting transfers between devices  2.75 us (1%)
    ppermute x3, waiting for transfers between devices, per_device(): lax.ppermute(state, 'pp', [(n_pp - 1, dst)])  108 us
    pallas_call x1, Pallas kernels, run_layer(): pl.pallas_call(functools.partial(layer_kernel, dims), out_shape=(jax.Shap...  62.6 us
    select_n x1, other arithmetic, per_device(): value_t = jnp.where(row_hit, value_new[:, :, None], value_t)  23 us
  transfers between devices with their start and end apart: 3, of which 1 were waited for; matrix products, arithmetic and copies ran while one was open for 12% of the time, Pallas kernels for 0%

profile of v2, /device:TPU:0, one launch (start us, length us, event | category | flops | bytes accessed | tf_op | source)
XLA Modules:
  0.0 201.3 jit_solution(3002085740361702579)
XLA Ops:
  0.7 0.7 convert_element_type.3
  1.3 0.8 multiply_sine_fusion
  2.2 62.6 %layer.1 = (bf16[2,128,2048]{2,1,0:T(8,128)(2,1)}, bf16[2,16,64,128]{3,2,1,0:T(8,128)(2,1)}, bf16[2,16,64,128]{3,2,1,0:T(8,128)(2,1)}) custom-call(f32[2,32,128]{2,1,0:T(8,128)} %get-tuple-element.12.cos_ref, f32[2,32,128]{2,1,0:T(8,128)} %get-tuple-element.11.sin_ref, s32[2,1,128]{2,1,0:T(1,128)} %bitcast.27, bf16[1,2048]{1,0:T(2,128)(2,1)} %ga_ref.1, ...), custom_call_target="tpu_custom_call" | custom-call | tf_op jit(solution)/shard_map/layer/pallas_call | solution.py:302
  64.7 0.7 collective-permute-start.2
  65.5 0.7 collective-permute-start.1
  66.2 1.3 collective-permute-start
  67.5 0.7 iota_compare_fusion
  68.2 0.0 copy-start
  68.2 23.0 %broadcast_select_fusion = (bf16[1,2,128,16,32,64]{2,5,4,3,1,0:T(8,128)(2,1)}, bf16[1,2,128,16,32,64]{2,5,4,3,1,0:T(8,128)(2,1)}) fusion(bf16[1,2,128,16,32,64]{2,5,4,3,1,0:T(8,128)(2,1)} %param.16, pred[2,128,32]{1,2,0:T(8,128)(4,1)S(1)} %iota_compare_fusion, bf16[2,128,16,64]{1,3,2,0:T(8,128)(2,1)} %bitcast.26, bf16[1,2,128,16,32,64]{2,5,4,3,1,0:T(8,128)(2,1)} %param.15, ...), kind=kLoop, calls=%fused_computation | loop fusion | flops 16777216 | bytes 68165632 | tf_op jit(solution)/shard_map/jit(_where)/select_n | solution.py:359
  91.2 0.0 collective-permute-done.2
  91.2 0.0 collective-permute-done.1
  91.2 107.7 %collective-permute-done = bf16[2,128,2048]{2,1,0:T(8,128)(2,1)} collective-permute-done((bf16[2,128,2048]{2,1,0:T(8,128)(2,1)}, bf16[2,128,2048]{2,1,0:T(8,128)(2,1)}, u32[]{:S(2)}, u32[]{:S(2)}) %collective-permute-start) | collective-permute-done | bytes 1048608 | tf_op jit(solution)/shard_map/ppermute | solution.py:354
  198.9 0.0 copy-done
  198.9 2.4 %add_select_fusion = bf16[2,128,2048]{2,1,0:T(8,128)(2,1)} fusion(bf16[2,128,2048]{2,1,0:T(8,128)(2,1)S(1)} %copy-done, bf16[2,128,2048]{2,1,0:T(8,128)(2,1)S(1)} %collective-permute-done.2, bf16[2,128,2048]{2,1,0:T(8,128)(2,1)} %collective-permute-done, bf16[2,128,2048]{2,1,0:T(8,128)(2,1)S(1)} %collective-permute-done.1, pred[]{:T(512)S(6)} %eq.22), kind=kLoop, calls=%fused_computation.2 | loop fusion | flops 1572864 | bytes 5242881 | tf_op jit(solution)/shard_map/jit(_where)/select_n | solution.py:355
  (1 shorter events, 0.0 us)
Async XLA Ops:
  64.7 26.5 %collective-permute-start.2 = (bf16[2,128,2048]{2,1,0:T(8,128)(2,1)}, bf16[2,128,2048]{2,1,0:T(8,128)(2,1)S(1)}, u32[]{:S(2)}, u32[]{:S(2)}) collective-permute-start(bf16[2,128,2048]{2,1,0:T(8,128)(2,1)} %get-tuple-element.6), channel_id=1, source_target_pairs={{3,2},{7,6}} | collective-permute-start | bytes 3145736 | tf_op jit(solution)/shard_map/ppermute | solution.py:354
  65.5 25.7 %collective-permute-start.1 = (bf16[2,128,2048]{2,1,0:T(8,128)(2,1)}, bf16[2,128,2048]{2,1,0:T(8,128)(2,1)S(1)}, u32[]{:S(2)}, u32[]{:S(2)}) collective-permute-start(bf16[2,128,2048]{2,1,0:T(8,128)(2,1)} %get-tuple-element.6), channel_id=1, source_target_pairs={{3,1},{7,5}} | collective-permute-start | bytes 3145736 | tf_op jit(solution)/shard_map/ppermute | solution.py:354
  66.2 132.7 %collective-permute-start = (bf16[2,128,2048]{2,1,0:T(8,128)(2,1)}, bf16[2,128,2048]{2,1,0:T(8,128)(2,1)}, u32[]{:S(2)}, u32[]{:S(2)}) collective-permute-start(bf16[2,128,2048]{2,1,0:T(8,128)(2,1)} %get-tuple-element.6), channel_id=1, source_target_pairs={{3,0},{7,4}} | collective-permute-start | bytes 3145736 | tf_op jit(solution)/shard_map/ppermute | solution.py:354
  68.2 130.7 %copy-start = (bf16[2,128,2048]{2,1,0:T(8,128)(2,1)S(1)}, bf16[2,128,2048]{2,1,0:T(8,128)(2,1)}, u32[]{:S(2)}) copy-start(bf16[2,128,2048]{2,1,0:T(8,128)(2,1)} %get-tuple-element.6) | copy-start | bytes 3145732

commit v3 on v2

--- a/solution.py
+++ b/solution.py
@@ -21,6 +21,8 @@
 ROWS = 1024
 SLOTS = 8
 NORM_ROWS = 32
+KEEP_SLOTS = 16
+WRITE_SLOTS = 24
 
 
 def rope_freqs(head_dim):
@@ -33,7 +35,7 @@
     return jnp.where(wave_len < ORIG_CONTEXT / HIGH_FACTOR, base_freq, long_freq)
 
 
-def layer_kernel(dims, cos_ref, sin_ref, pos_ref, ga_ref, gm_ref, hid, kc, vc, wq, wk, wv, wo, wg, wu, wd,
+def layer_kernel(dims, after, cos_ref, sin_ref, pos_ref, ga_ref, gm_ref, hid, kc, vc, wq, wk, wv, wo, wg, wu, wd,
                  hout, knew, vnew,
                  wqkv_v, wo_v, wg_v, wu_v, ring, hbuf, recvp, recvd, nbuf, qt, ubuf, sc,
                  hid_sem, wqkv_sem, wo_sem, gu_sem, ring_sem,
@@ -70,7 +72,7 @@
             ring.at[slot, pl.ds(i * deep, deep)], ring_sem.at[slot, i]) for i in range(slabs)]
 
     def gu_copies(j):
-        cols = pl.ds(j * COLS, COLS)
+        cols = pl.ds(pl.multiple_of(j * COLS, COLS), COLS)
         return (pltpu.make_async_copy(wg.at[:, cols], wg_v.at[j], gu_sem.at[0, j]),
                 pltpu.make_async_copy(wu.at[:, cols], wu_v.at[j], gu_sem.at[1, j]))
 
@@ -104,21 +106,40 @@
             hid_copy(g).start()
     for copy in qkv_copies():
         copy.start()
-    for slot in range(SLOTS):
-        for copy in kv_copies(slot, slot):
-            copy.start()
-    wo_copy().start()
+
+    def start_kv_wo():
+        for slot in range(SLOTS):
+            for copy in kv_copies(slot, slot):
+                copy.start()
+        wo_copy().start()
+
+    @pl.when(pp > 0)
+    def _():
+        start_kv_wo()
+        for j in range(n_gu):
+            for copy in gu_copies(j):
+                copy.start()
 
     barrier = pltpu.get_barrier_semaphore()
-    for other in (peer, nxt, prv):
-        pl.semaphore_signal(barrier, inc=1, device_id=other, device_id_type=MESH)
-    pl.semaphore_wait(barrier, 3)
-
-    for copy in qkv_copies():
-        copy.wait()
-    for j in range(n_gu):
-        for copy in gu_copies(j):
-            copy.start()
+    pl.semaphore_signal(barrier, inc=1, device_id=peer, device_id_type=MESH)
+
+    @pl.when(jnp.logical_not(last))
+    def _():
+        pl.semaphore_signal(barrier, inc=1, device_id=nxt, device_id_type=MESH)
+
+    @pl.when(pp > 0)
+    def _():
+        pl.semaphore_signal(barrier, inc=1, device_id=prv, device_id_type=MESH)
+    ends = jnp.logical_or(first, last)
+
+    @pl.when(ends)
+    def _():
+        pl.semaphore_wait(barrier, 2)
+
+    @pl.when(jnp.logical_not(ends))
+    def _():
+        pl.semaphore_wait(barrier, 3)
+
     def norm_rows(g, gain_ref, with_partial):
         def body(r, carry):
             rows = pl.ds(pl.multiple_of(r * NORM_ROWS, NORM_ROWS), NORM_ROWS)
@@ -148,6 +169,13 @@
         sine = sin_ref[g]
         half = hd // 2
         for which in range(3):
+            @pl.when(g == 0)
+            def _():
+                qkv_copies()[which].wait()
+            if which == 0:
+                @pl.when(jnp.logical_and(first, g == 0))
+                def _():
+                    start_kv_wo()
             for c in range(hw // COLS):
                 cols = slice(c * COLS, (c + 1) * COLS)
                 prod = jnp.dot(nbuf[...], wqkv_v[which, :, cols], preferred_element_type=F32)
@@ -198,6 +226,11 @@
                 for copy in kv_copies(item + SLOTS, slot):
                     copy.start()
 
+            @pl.when(jnp.logical_and(first, lax.rem(item, SLOTS) == SLOTS - 1))
+            def _():
+                for copy in gu_copies(item // SLOTS):
+                    copy.start()
+
             @pl.when(item + SLOTS >= n_kv)
             def _():
                 for copy in wd_copies(item + SLOTS, slot):
@@ -220,6 +253,12 @@
         return carry
 
     def mlp_phase(g, carry):
+        @pl.when(jnp.logical_and(first, g == 0))
+        def _():
+            for j in range(n_kv // SLOTS, n_gu):
+                for copy in gu_copies(j):
+                    copy.start()
+
         for c in range(n_chunk):
             p_copy(g, c).wait()
         norm_rows(g, gm_ref, True)
@@ -304,7 +343,7 @@
         out_shape=(jax.ShapeDtypeStruct((n_groups, n_batch, d_model), BF16),
                    jax.ShapeDtypeStruct((n_groups, heads, hd, n_batch), BF16),
                    jax.ShapeDtypeStruct((n_groups, heads, hd, n_batch), BF16)),
-        in_specs=[vmem] * 5 + [hbm] * 10,
+        in_specs=[hbm] + [vmem] * 5 + [hbm] * 10,
         out_specs=(vmem, vmem, vmem),
         scratch_shapes=[
             pltpu.VMEM((3, d_model, hw), BF16),
@@ -328,6 +367,179 @@
     )(*args)
 
 
+def keep_kernel(dims, pos, kc, vc, kout, vout, todo, kb, vb, flags, in_sem, out_sem):
+    n_groups, n_batch, _, heads, seq, _, _, n_pp, _ = dims
+    n_slab = n_groups * seq
+    n_items = n_groups * heads
+    ahead = KEEP_SLOTS // 2
+    last = lax.axis_index("pp") == n_pp - 1
+
+    def loads(i):
+        slot = lax.rem(i, KEEP_SLOTS)
+        g, h = i // heads, lax.rem(i, heads)
+        return (pltpu.make_async_copy(kc.at[g, h], kb.at[slot], in_sem.at[0, slot]),
+                pltpu.make_async_copy(vc.at[g, h], vb.at[slot], in_sem.at[1, slot]))
+
+    def stores(i):
+        slot = lax.rem(i, KEEP_SLOTS)
+        g, h = i // heads, lax.rem(i, heads)
+        return (pltpu.make_async_copy(kb.at[slot], kout.at[g, h], out_sem.at[0, slot]),
+                pltpu.make_async_copy(vb.at[slot], vout.at[g, h], out_sem.at[1, slot]))
+
+    @pl.when(jnp.logical_not(last))
+    def _():
+        todo[0] = n_slab
+
+        def number(i, carry):
+            todo[i + 1] = i
+            return carry
+        lax.fori_loop(0, n_slab, number, 0)
+
+    @pl.when(last)
+    def _():
+        for i in range(ahead):
+            for copy in loads(i):
+                copy.start()
+
+        def clear(i, carry):
+            flags[i] = 0
+            todo[i + 1] = 0
+            return carry
+        lax.fori_loop(0, n_slab, clear, 0)
+        for g in range(n_groups):
+            def mark(b, carry):
+                flags[g * seq + pos[g, b]] = 1
+                return carry
+            lax.fori_loop(0, n_batch, mark, 0)
+
+        def pick(i, count):
+            hit = flags[i]
+
+            @pl.when(hit == 1)
+            def _():
+                todo[count + 1] = i
+            return count + hit
+        todo[0] = lax.fori_loop(0, n_slab, pick, jnp.int32(0))
+
+        def body(i, carry):
+            for copy in loads(i):
+                copy.wait()
+            for copy in stores(i):
+                copy.start()
+
+            @pl.when(i + ahead < n_items)
+            def _():
+                @pl.when(i >= ahead)
+                def _():
+                    for copy in stores(i - ahead):
+                        copy.wait()
+                for copy in loads(i + ahead):
+                    copy.start()
+            return carry
+        lax.fori_loop(0, n_items, body, 0)
+        for i in range(n_items - 2 * ahead, n_items):
+            for copy in stores(i):
+                copy.wait()
+
+
+def keep_old(dims, positions, key_t, value_t):
+    n_groups, n_batch, _, heads, seq, hd, _, _, _ = dims
+    hbm = pl.BlockSpec(memory_space=pl.ANY)
+    smem = pl.BlockSpec(memory_space=pltpu.SMEM)
+    dma = pltpu.SemaphoreType.DMA
+    return pl.pallas_call(
+        functools.partial(keep_kernel, dims),
+        out_shape=(jax.ShapeDtypeStruct(key_t.shape, BF16), jax.ShapeDtypeStruct(value_t.shape, BF16),
+                   jax.ShapeDtypeStruct((n_groups * seq + 1,), jnp.int32)),
+        in_specs=[smem, hbm, hbm],
+        out_specs=(hbm, hbm, smem),
+        scratch_shapes=[
+            pltpu.VMEM((KEEP_SLOTS, seq, hd, n_batch), BF16),
+            pltpu.VMEM((KEEP_SLOTS, seq, hd, n_batch), BF16),
+            pltpu.SMEM((n_groups * seq,), jnp.int32),
+            dma((2, KEEP_SLOTS)), dma((2, KEEP_SLOTS)),
+        ],
+        compiler_params=pltpu.CompilerParams(vmem_limit_bytes=40 * 2**20),
+        name="cache_keep",
+    )(positions, key_t, value_t)
+
+
+def write_kernel(dims, todo, pos_ref, knew, vnew, kc, vc, kold, vold, kout, vout, kb, vb, in_sem, out_sem):
+    _, _, _, _, seq, _, _, _, _ = dims
+    ahead = WRITE_SLOTS // 2
+    count = todo[0]
+
+    def place(i):
+        entry = todo[i + 1]
+        return entry // seq, lax.rem(entry, seq), lax.rem(i, WRITE_SLOTS)
+
+    def loads(i):
+        g, s, slot = place(i)
+        return (pltpu.make_async_copy(kc.at[g, :, s], kb.at[slot], in_sem.at[0, slot]),
+                pltpu.make_async_copy(vc.at[g, :, s], vb.at[slot], in_sem.at[1, slot]))
+
+    def stores(i):
+        g, s, slot = place(i)
+        return (pltpu.make_async_copy(kb.at[slot], kout.at[g, :, s], out_sem.at[0, slot]),
+                pltpu.make_async_copy(vb.at[slot], vout.at[g, :, s], out_sem.at[1, slot]))
+
+    for i in range(ahead):
+        @pl.when(i < count)
+        def _():
+            for copy in loads(i):
+                copy.start()
+
+    def body(i, carry):
+        g, s, slot = place(i)
+        for copy in loads(i):
+            copy.wait()
+        hit = (pos_ref[g] == s)[None]
+        for new, buf in ((knew, kb), (vnew, vb)):
+            buf[slot] = jnp.where(hit, new[g].astype(F32), buf[slot].astype(F32)).astype(BF16)
+        for copy in stores(i):
+            copy.start()
+
+        @pl.when(i + ahead < count)
+        def _():
+            @pl.when(i >= ahead)
+            def _():
+                for copy in stores(i - ahead):
+                    copy.wait()
+            for copy in loads(i + ahead):
+                copy.start()
+        return carry
+    lax.fori_loop(0, count, body, 0)
+
+    def drain(i, carry):
+        for copy in stores(i):
+            copy.wait()
+        return carry
+    lax.fori_loop(jnp.maximum(count - 2 * ahead, 0), count, drain, 0)
+
+
+def write_new(dims, todo, pos, key_new, value_new, key_t, value_t, key_old, value_old):
+    n_groups, n_batch, _, heads, seq, hd, _, _, _ = dims
+    hbm = pl.BlockSpec(memory_space=pl.ANY)
+    vmem = pl.BlockSpec(memory_space=pltpu.VMEM)
+    smem = pl.BlockSpec(memory_space=pltpu.SMEM)
+    dma = pltpu.SemaphoreType.DMA
+    return pl.pallas_call(
+        functools.partial(write_kernel, dims),
+        out_shape=(jax.ShapeDtypeStruct(key_t.shape, BF16), jax.ShapeDtypeStruct(value_t.shape, BF16)),
+        in_specs=[smem, vmem, vmem, vmem, hbm, hbm, hbm, hbm],
+        out_specs=(hbm, hbm),
+        scratch_shapes=[
+            pltpu.VMEM((WRITE_SLOTS, heads, hd, n_batch), BF16),
+            pltpu.VMEM((WRITE_SLOTS, heads, hd, n_batch), BF16),
+            dma((2, WRITE_SLOTS)), dma((2, WRITE_SLOTS)),
+        ],
+        input_output_aliases={6: 0, 7: 1},
+        compiler_params=pltpu.CompilerParams(vmem_limit_bytes=40 * 2**20),
+        cost_estimate=pl.CostEstimate(flops=n_groups * n_batch * heads * seq * hd * 40, bytes_accessed=8 * key_t.size, transcendentals=0),
+        name="cache_write",
+    )(todo, pos, key_new, value_new, key_t, value_t, key_old, value_old)
+
+
 def solution(mesh):
     n_pp = mesh.shape["pp"]
     n_tp = mesh.shape["tp"]
@@ -346,17 +558,18 @@
         angles = positions.astype(F32)[:, None, :] * rope_freqs(hd)[None, :, None]
         key_t = jnp.transpose(key_cache[0], (0, 2, 3, 4, 1))
         value_t = jnp.transpose(value_cache[0], (0, 2, 3, 4, 1))
+        pos = positions[:, None, :]
+        key_old, value_old, todo = keep_old(dims, positions, key_t, value_t)
         state, key_new, value_new = run_layer(
-            dims, jnp.cos(angles), jnp.sin(angles), positions[:, None, :], attn_norm, mlp_norm, hidden, key_t, value_t,
+            dims, todo, jnp.cos(angles), jnp.sin(angles), pos, attn_norm, mlp_norm, hidden, key_t, value_t,
             w_query[0], w_key[0], w_value[0], w_out[0], w_gate[0], w_up[0], w_down[0].reshape(ff // hd, hd, d_model))
 
         stage = lax.axis_index("pp")
-        from_last = [lax.ppermute(state, "pp", [(n_pp - 1, dst)]) for dst in range(n_pp - 1)]
+        from_last = [lax.ppermute(state, "pp", [(n_pp - 1, dst)]) for dst in range(1, n_pp - 1)]
+        key_t, value_t = write_new(dims, todo, pos, key_new, value_new, key_t, value_t, key_old, value_old)
+        from_last[0], key_t = lax.optimization_barrier((from_last[0], key_t))
+        from_last.append(lax.ppermute(from_last[0], "pp", [(1, 0)]))
         final = jnp.where(stage == n_pp - 1, state, sum(from_last[1:], from_last[0]))
-
-        row_hit = jnp.arange(seq, dtype=jnp.int32)[None, None, :, None, None] == positions[:, None, None, None, :]
-        key_t = jnp.where(row_hit, key_new[:, :, None], key_t)
-        value_t = jnp.where(row_hit, value_new[:, :, None], value_t)
         return final, jnp.transpose(key_t, (0, 4, 1, 2, 3))[None], jnp.transpose(value_t, (0, 4, 1, 2, 3))[None]
 
     return jax.shard_map(per_device, mesh=mesh, in_specs=in_specs, out_specs=out_specs, check_vma=False)

time: 202 us -> 193 us (0.955)
  other arithmetic: 27.6 us -> 3.92 us
  Pallas kernels: 62.6 us -> 83.2 us
  waiting for transfers between devices: 108 us -> 96.7 us
  local copies, waits for them, and re-layouts: 0.01 us -> 4.53 us
    ppermute x3 -> x2, waiting for transfers between devices: 108 us -> 0.01 us  [per_device(): lax.ppermute(state, 'pp', [(n_pp - 1, dst)])]
    ppermute x0 -> x1, waiting for transfers between devices: none -> 96.6 us  [per_device(): from_last.append(lax.ppermute(from_last[0], 'pp', [(1, 0)]))]
    pallas_call x0 -> x2, Pallas kernels: none -> 25.8 us  [the longest x1 23.7 us: write_new(): pl.pallas_call(functools.partial(write_kernel, dims), out_shape=(jax.Shap...]
    select_n x1 -> x0, other arithmetic: 23 us -> none  [per_device(): value_t = jnp.where(row_hit, value_new[:, :, None], value_t)]
    pallas_call x1, Pallas kernels: 62.6 us -> 57.4 us  [run_layer(): pl.pallas_call(functools.partial(layer_kernel, dims), out_shape=(jax.Shap...]
    unnamed x2 -> x14, local copies, waits for them, and re-layouts: 0.01 us -> 4.53 us
  transfers between devices with their start and end apart: 3 -> 3, of which waited for: 1 -> 1; matrix products, arithmetic and copies ran while one was open for 12% -> 0% of each run, Pallas kernels for 0% -> 12%
where the time goes in v3:
time: 193 us; the launch traced here: 192 us
  waiting for transfers between devices  96.7 us (50%)
  Pallas kernels  83.2 us (43%)
  local copies, waits for them, and re-layouts  4.53 us (2%)
  other arithmetic  3.92 us (2%)
  starting transfers between devices  2.75 us (1%)
    ppermute x1, waiting for transfers between devices, per_device(): from_last.append(lax.ppermute(from_last[0], 'pp', [(1, 0)]))  96.6 us
    pallas_call x1, Pallas kernels, run_layer(): pl.pallas_call(functools.partial(layer_kernel, dims), out_shape=(jax.Shap...  57.4 us
    pallas_call x1, Pallas kernels, write_new(): pl.pallas_call(functools.partial(write_kernel, dims), out_shape=(jax.Shap...  23.7 us
    unnamed x14, local copies, waits for them, and re-layouts  4.53 us
  transfers between devices with their start and end apart: 3, of which 1 were waited for; matrix products, arithmetic and copies ran while one was open for 0% of the time, Pallas kernels for 12%

profile of v3, /device:TPU:0, one launch (start us, length us, event | category | flops | bytes accessed | tf_op | source)
XLA Modules:
  0.0 191.8 jit_solution(14974748587635000777)
XLA Ops:
  0.7 0.7 convert_element_type.3
  1.3 0.0 copy-start.2
  1.3 0.7 copy-done.2
  2.0 2.1 %cache_keep.1 = (bf16[2,16,32,64,128]{4,3,2,1,0:T(8,128)(2,1)}, bf16[2,16,32,64,128]{4,3,2,1,0:T(8,128)(2,1)}, s32[65]{0:T(128)S(1)}) custom-call(s32[2,128]{1,0:T(2,128)S(1)} %copy-done.2, bf16[2,16,32,64,128]{4,3,2,1,0:T(8,128)(2,1)} %bitcast.22, bf16[2,16,32,64,128]{4,3,2,1,0:T(8,128)(2,1)} %bitcast.25), custom_call_target="tpu_custom_call" | custom-call | tf_op jit(solution)/shard_map/cache_keep/pallas_call | solution.py:450
  4.2 0.0 copy-start.4
  4.2 0.5 copy-done.4
  4.7 0.8 multiply_sine_fusion
  5.5 57.4 %layer.1 = (bf16[2,128,2048]{2,1,0:T(8,128)(2,1)}, bf16[2,16,64,128]{3,2,1,0:T(8,128)(2,1)}, bf16[2,16,64,128]{3,2,1,0:T(8,128)(2,1)}) custom-call(s32[65]{0:T(128)} %copy-done.4, f32[2,32,128]{2,1,0:T(8,128)} %get-tuple-element.24.cos_ref, f32[2,32,128]{2,1,0:T(8,128)} %get-tuple-element.23.sin_ref, s32[2,1,128]{2,1,0:T(1,128)} %bitcast.20, ...), custom_call_target="tpu_custom_call" | custom-call | tf_op jit(solution)/shard_map/layer/pallas_call | solution.py:341
  62.9 0.7 collective-permute-start
  63.6 0.7 collective-permute-start.1
  64.4 0.0 copy-start
  64.4 1.0 copy-done
  65.4 0.0 copy-start.1
  65.4 1.0 copy-done.1
  66.5 0.0 copy-start.3
  66.5 0.7 copy-done.3
  67.1 0.0 copy-start.5
  67.1 0.6 copy-done.5
  67.7 0.0 copy-start.6
  67.7 23.7 %cache_write.1 = (bf16[2,16,32,64,128]{4,3,2,1,0:T(8,128)(2,1)}, bf16[2,16,32,64,128]{4,3,2,1,0:T(8,128)(2,1)}) custom-call(s32[65]{0:T(128)S(1)} %copy-done.5, s32[2,1,128]{2,1,0:T(1,128)S(1)} %bitcast.21, bf16[2,16,64,128]{3,2,1,0:T(8,128)(2,1)S(1)} %copy-done, ...), custom_call_target="tpu_custom_call", output_to_operand_aliasing={{0}: (6, {}), {1}: (7, {})} | custom-call | flops 335544320 | bytes 67108864 | tf_op jit(solution)/shard_map/cache_write/pallas_call | solution.py:526
  91.4 0.0 collective-permute-done
  91.4 1.3 collective-permute-start.2
  92.7 0.0 collective-permute-done.1
  92.7 96.6 %collective-permute-done.2 = bf16[2,128,2048]{2,1,0:T(8,128)(2,1)} collective-permute-done((bf16[2,128,2048]{2,1,0:T(8,128)(2,1)S(1)}, bf16[2,128,2048]{2,1,0:T(8,128)(2,1)}, u32[]{:S(2)}, u32[]{:S(2)}) %collective-permute-start.2) | collective-permute-done | bytes 1048608 | tf_op jit(solution)/shard_map/ppermute | solution.py:571
  189.4 0.0 copy-done.6
  189.4 2.4 %add_select_fusion = bf16[2,128,2048]{2,1,0:T(8,128)(2,1)} fusion(bf16[2,128,2048]{2,1,0:T(8,128)(2,1)S(1)} %copy-done.6, bf16[2,128,2048]{2,1,0:T(8,128)(2,1)} %collective-permute-done.2, bf16[2,128,2048]{2,1,0:T(8,128)(2,1)S(1)} %collective-permute-done, bf16[2,128,2048]{2,1,0:T(8,128)(2,1)S(1)} %collective-permute-done.1, pred[]{:T(512)S(6)} %eq.3), kind=kLoop, calls=%fused_computation | loop fusion | flops 1572864 | bytes 5242881 | tf_op jit(solution)/shard_map/jit(_where)/select_n | solution.py:572
  (1 shorter events, 0.0 us)
Async XLA Ops:
  1.3 0.7 copy-start.2
  4.2 0.5 copy-start.4
  62.9 28.5 %collective-permute-start = (bf16[2,128,2048]{2,1,0:T(8,128)(2,1)}, bf16[2,128,2048]{2,1,0:T(8,128)(2,1)S(1)}, u32[]{:S(2)}, u32[]{:S(2)}) collective-permute-start(bf16[2,128,2048]{2,1,0:T(8,128)(2,1)} %get-tuple-element.14), channel_id=1, source_target_pairs={{3,1},{7,5}} | collective-permute-start | bytes 3145736 | tf_op jit(solution)/shard_map/ppermute | solution.py:568
  63.6 29.1 %collective-permute-start.1 = (bf16[2,128,2048]{2,1,0:T(8,128)(2,1)}, bf16[2,128,2048]{2,1,0:T(8,128)(2,1)S(1)}, u32[]{:S(2)}, u32[]{:S(2)}) collective-permute-start(bf16[2,128,2048]{2,1,0:T(8,128)(2,1)} %get-tuple-element.14), channel_id=1, source_target_pairs={{3,2},{7,6}} | collective-permute-start | bytes 3145736 | tf_op jit(solution)/shard_map/ppermute | solution.py:568
  64.4 1.0 copy-start
  65.4 1.0 copy-start.1
  66.5 0.7 copy-start.3
  67.1 0.6 copy-start.5
  67.7 121.6 %copy-start.6 = (bf16[2,128,2048]{2,1,0:T(8,128)(2,1)S(1)}, bf16[2,128,2048]{2,1,0:T(8,128)(2,1)}, u32[]{:S(2)}) copy-start(bf16[2,128,2048]{2,1,0:T(8,128)(2,1)} %get-tuple-element.14) | copy-start | bytes 3145732
  91.4 98.0 %collective-permute-start.2 = (bf16[2,128,2048]{2,1,0:T(8,128)(2,1)S(1)}, bf16[2,128,2048]{2,1,0:T(8,128)(2,1)}, u32[]{:S(2)}, u32[]{:S(2)}) collective-permute-start(bf16[2,128,2048]{2,1,0:T(8,128)(2,1)S(1)} %collective-permute-done), channel_id=1, source_target_pairs={{1,0},{5,4}} | collective-permute-start | bytes 3145736 | tf_op jit(solution)/shard_map/ppermute | solution.py:571
